TPU v7x, 32 devices: a whole 2x2x4 slice. The times are simulated.
32 devices in a mesh: row: 4 (over y, core), col: 8 (over z, x).
Axes of the slice: x: 2, y: 2, z: 4, core: 2. Of those that a mesh axis runs over, the one named last changes fastest.
Arguments:
- start_field: float32 [1, 2, 4096, 8192], P(None, None, 'col', 'row'), may hold values from -6 to 6
- section_field: float32 [1, 2, 4096, 8192], P(None, None, 'col', 'row'), may hold values from -26 to 26
- start_term: float32 [1, 2, 4096, 8192], P(None, None, 'col', 'row'), may hold values from -6 to 6
- first_term: float32 [1, 2, 4096, 8192], P(None, None, 'col', 'row'), may hold values from -6 to 6
- second_term: float32 [1, 2, 4096, 8192], P(None, None, 'col', 'row'), may hold values from -6 to 6
Outputs:
- next_field: float32 [1, 2, 4096, 8192], P(None, None, 'col', 'row')
All inputs are finite; a program needn't handle non-finite values.
Results may differ from a plain program's by a relative error of at most 0.0001.
Values sent between devices are 32-bit elements; how exact they have to be, the bound alone decides.
A program may use at most 256 MiB of HBM per device.

v0:
```python
import math

import jax
import jax.numpy as jnp
from jax import lax
from jax.sharding import PartitionSpec as P

RADIX = 128


viscous_rate = 1.5
wave_scale = 3.0
series_terms = 12


def section_weights(wave_x, wave_y, length):
    square = wave_x * wave_x + wave_y * wave_y
    kappa_x = wave_scale * wave_x.astype(jnp.float32) / length
    kappa_y = wave_scale * wave_y.astype(jnp.float32) / length
    kappa_sq = kappa_x * kappa_x + kappa_y * kappa_y
    zvalue = -viscous_rate * kappa_sq
    damping = jnp.exp(zvalue)
    near_zero = 27 * square < 2 * length * length

    def series(degree):
        running = jnp.full_like(zvalue, 1.0 / math.factorial(series_terms - 1 + degree))
        for term_index in range(series_terms - 2, -1, -1):
            running = running * zvalue + 1.0 / math.factorial(term_index + degree)
        return running

    clamped = jnp.where(near_zero, -1.0, zvalue)
    exp_clamped = jnp.exp(clamped)
    closed_one = (exp_clamped - 1.0) / clamped
    closed_two = (exp_clamped - 1.0 - clamped) / (clamped * clamped)
    closed_three = (exp_clamped - 1.0 - clamped - 0.5 * clamped * clamped) / (
        clamped * clamped * clamped
    )
    phi_one = jnp.where(near_zero, series(1), closed_one)
    phi_two = jnp.where(near_zero, series(2), closed_two)
    phi_three = jnp.where(near_zero, series(3), closed_three)
    weight_a = phi_one - 3.0 * phi_two + 4.0 * phi_three
    weight_b = phi_two - 2.0 * phi_three
    weight_c = 4.0 * phi_three - phi_two
    keep_mask = ((3 * jnp.abs(wave_x) < length) & (3 * jnp.abs(wave_y) < length)).astype(
        jnp.float32
    )
    inverse_sq = length * length / (9.0 * jnp.maximum(square, 1).astype(jnp.float32))
    return (damping, weight_a, weight_b, weight_c, kappa_x, kappa_y, keep_mask, inverse_sq)


def section_table(count_in, count_out, period, direction):
    row_ids = lax.broadcasted_iota(jnp.int32, (count_in, count_out), 0)
    col_ids = lax.broadcasted_iota(jnp.int32, (count_in, count_out), 1)
    angles = direction * 2.0 * math.pi / period * (row_ids * col_ids % period).astype(jnp.float32)
    cosine = jnp.cos(angles)
    sine_part = jnp.sin(angles)
    return jnp.stack(
        [jnp.stack([cosine, sine_part], axis=1), jnp.stack([-sine_part, cosine], axis=1)], axis=0
    )


def twiddle(count_c, count_b, period, direction):
    row_ids = lax.broadcasted_iota(jnp.int32, (count_c, count_b), 0)
    col_ids = lax.broadcasted_iota(jnp.int32, (count_c, count_b), 1)
    angles = direction * 2.0 * math.pi / period * (row_ids * col_ids % period).astype(jnp.float32)
    return (jnp.cos(angles), jnp.sin(angles))


def rotate(values, cosine, sine_part):
    return jnp.stack(
        [values[0] * cosine - values[1] * sine_part, values[0] * sine_part + values[1] * cosine]
    )


def back_rows(values):
    return lax.all_to_all(values, "row", split_axis=3, concat_axis=2, tiled=True)


def row_pass(batched, transform):
    return transform(lax.all_to_all(batched, "row", split_axis=2, concat_axis=3, tiled=True))


def rows_inverse(pieces):
    count_a = pieces.shape[3]
    count_b = pieces.shape[4]
    section_one = jnp.einsum(
        "pnkab,pasc->snkcb",
        pieces,
        section_table(count_a, count_a, count_a, 1.0),
        precision=lax.Precision.HIGHEST,
    )
    cosine, sine_part = twiddle(count_a, count_b, count_a * count_b, 1.0)
    section_one = rotate(section_one, cosine, sine_part)
    section_two = jnp.einsum(
        "pnkcb,pbsd->snkcd",
        section_one,
        section_table(count_b, count_b, count_b, 1.0),
        precision=lax.Precision.HIGHEST,
    )
    return back_rows(section_two)


def cols_inverse(pieces):
    half_count = pieces.shape[4]
    count_b = RADIX
    count_a = half_count // count_b
    count_c = 2 * count_a
    period = 2 * half_count
    weights = jnp.where(lax.broadcasted_iota(jnp.int32, (half_count,), 0) == 0, 1.0, 2.0)
    shaped = (pieces * weights).reshape(pieces.shape[:4] + (count_a, count_b))
    section_one = jnp.einsum(
        "pnyzab,pasc->snyzcb",
        shaped,
        section_table(count_a, count_c, count_c, 1.0),
        precision=lax.Precision.HIGHEST,
    )
    cosine, sine_part = twiddle(count_c, count_b, period, 1.0)
    section_one = rotate(section_one, cosine, sine_part)
    real_table = section_table(count_b, count_b, count_b, 1.0)[:, :, 0, :]
    real_grid = jnp.einsum(
        "pnyzcb,pbd->nyzcd", section_one, real_table, precision=lax.Precision.HIGHEST
    )
    return real_grid * (1.0 / period)


def rows_forward(pieces):
    count_c = pieces.shape[3]
    count_d = pieces.shape[4]
    section_one = jnp.einsum(
        "pnkcd,pdsf->snkcf",
        pieces,
        section_table(count_d, count_d, count_d, -1.0),
        precision=lax.Precision.HIGHEST,
    )
    cosine, sine_part = twiddle(count_c, count_d, count_c * count_d, -1.0)
    section_one = rotate(section_one, cosine, sine_part)
    section_two = jnp.einsum(
        "pnkcf,pcse->snkef",
        section_one,
        section_table(count_c, count_c, count_c, -1.0),
        precision=lax.Precision.HIGHEST,
    )
    return back_rows(section_two)


def spectral_batch(spectra):
    real_stack = jnp.stack([couple[0] for couple in spectra])
    imag_stack = jnp.stack([couple[1] for couple in spectra])
    stacked = jnp.stack([real_stack, imag_stack])
    full_shape = stacked.shape
    return stacked.reshape(
        (2, full_shape[1] * full_shape[2], full_shape[3], full_shape[4] // RADIX, RADIX)
    )


def to_grid(batched):
    columns = row_pass(batched, rows_inverse)
    turned = jnp.transpose(columns, (0, 1, 3, 4, 2))
    return cols_inverse(lax.all_to_all(turned, "col", split_axis=3, concat_axis=4, tiled=True))


def to_spectrum(real_grid):
    count_c = real_grid.shape[3]
    count_d = real_grid.shape[4]
    period = count_c * count_d
    half_count = count_c // 2
    real_table = section_table(count_d, count_d, count_d, -1.0)[0]
    section_one = jnp.einsum(
        "nyzcd,dsf->snyzcf", real_grid, real_table, precision=lax.Precision.HIGHEST
    )
    cosine, sine_part = twiddle(count_c, count_d, period, -1.0)
    section_one = rotate(section_one, cosine, sine_part)
    section_two = jnp.einsum(
        "pnyzcf,pcse->snyzef",
        section_one,
        section_table(count_c, half_count, count_c, -1.0),
        precision=lax.Precision.HIGHEST,
    )
    flattened = section_two.reshape(section_two.shape[:4] + (half_count * count_d,))
    returned = lax.all_to_all(flattened, "col", split_axis=4, concat_axis=3, tiled=True)
    turned = jnp.transpose(returned, (0, 1, 4, 2, 3))
    spectral = row_pass(turned, rows_forward)
    return spectral.reshape(spectral.shape[:3] + (spectral.shape[3] * spectral.shape[4],)) * (
        1.0 / period
    )


def per_device(start_field, section_field, start_term, first_term, second_term):
    members = start_field.shape[0]
    block_x = start_field.shape[2]
    block_y = start_field.shape[3]
    length = block_y * lax.axis_size("row")
    wave_x = lax.axis_index("col") * block_x + lax.broadcasted_iota(
        jnp.int32, (block_x, block_y), 0
    )
    index_y = lax.axis_index("row") * block_y + lax.broadcasted_iota(
        jnp.int32, (block_x, block_y), 1
    )
    wave_y = jnp.where(index_y < length // 2, index_y, index_y - length)
    damping, weight_a, weight_b, weight_c, kappa_x, kappa_y, keep_mask, inverse_sq = (
        section_weights(wave_x, wave_y, length)
    )
    masked = section_field * keep_mask
    real_part = masked[:, 0]
    imag_part = masked[:, 1]
    psi_real = real_part * inverse_sq
    psi_imag = imag_part * inverse_sq
    vel_u = (-kappa_y * psi_imag, kappa_y * psi_real)
    vel_v = (kappa_x * psi_imag, -kappa_x * psi_real)
    spectra = [
        vel_u,
        vel_v,
        (-kappa_x * imag_part, kappa_x * real_part),
        (-kappa_y * imag_part, kappa_y * real_part),
    ]
    halfway = (len(spectra) + 1) // 2
    fields = jnp.concatenate(
        [to_grid(spectral_batch(spectra[:halfway])), to_grid(spectral_batch(spectra[halfway:]))],
        axis=0,
    )
    fields = fields.reshape((len(spectra), members) + fields.shape[1:])
    jacobian = fields[0] * fields[2] + fields[1] * fields[3]
    spectrum = to_spectrum(jacobian)
    jac_real = spectrum[0]
    jac_imag = spectrum[1]
    jac_both = jnp.stack([jac_real, jac_imag], axis=1)
    section_term = -keep_mask * jac_both
    return (
        damping * start_field
        + weight_a * start_term
        + 2.0 * weight_b * (first_term + second_term)
        + weight_c * section_term
    )


def solution(mesh):
    return jax.shard_map(
        per_device,
        mesh=mesh,
        in_specs=(
            P(None, None, "col", "row"),
            P(None, None, "col", "row"),
            P(None, None, "col", "row"),
            P(None, None, "col", "row"),
            P(None, None, "col", "row"),
        ),
        out_specs=P(None, None, "col", "row"),
        check_vma=False,
    )
```

profile of v0, /device:TPU:0, one launch (start us, length us, event | category | flops | bytes accessed | tf_op | source)
XLA Modules:
  0.0 2663.7 jit_solution(1795654685404084491)
XLA Ops:
  78.4 157.4 %all-to-all-done.3 = f32[2,2,512,16,128]{4,3,1,0,2:T(8,128)} async-done(((f32[2,2,512,16,128]{4,3,1,0,2:T(8,128)}), f32[2,2,512,16,128]{4,3,1,0,2:T(8,128)}, u32[]{:S(2)}, u32[]{:S(2)}) %all-to-all-start.3) | async-done | bytes 16777248 | tf_op jit(solution)/shard_map/all_to_all | solution.py:80
  256.5 169.8 %all-to-all-done = f32[2,2,512,16,128]{4,3,1,0,2:T(8,128)} async-done(((f32[2,2,512,16,128]{4,3,1,0,2:T(8,128)}), f32[2,2,512,16,128]{4,3,1,0,2:T(8,128)}, u32[]{:S(2)}, u32[]{:S(2)}) %all-to-all-start) | async-done | bytes 16777248 | tf_op jit(solution)/shard_map/all_to_all | solution.py:80
  510.7 24.0 fusion.41
  555.5 23.8 fusion.38
  585.6 145.9 %all-to-all-done.4 = f32[2,2,128,64,128]{2,4,1,0,3:T(8,128)} async-done(((f32[2,2,128,64,128]{2,4,1,0,3:T(8,128)}), f32[2,2,128,64,128]{2,4,1,0,3:T(8,128)}, u32[]{:S(2)}, u32[]{:S(2)}) %all-to-all-start.4) | async-done | bytes 16777248 | tf_op jit(solution)/shard_map/all_to_all | solution.py:76
  778.8 142.9 %all-to-all-done.1 = f32[2,2,128,64,128]{2,4,1,0,3:T(8,128)} async-done(((f32[2,2,128,64,128]{2,4,1,0,3:T(8,128)}), f32[2,2,128,64,128]{2,4,1,0,3:T(8,128)}, u32[]{:S(2)}, u32[]{:S(2)}) %all-to-all-start.1) | async-done | bytes 16777248 | tf_op jit(solution)/shard_map/all_to_all | solution.py:76
  968.5 322.5 %all-to-all-done.5 = f32[2,2,16,128,512]{4,2,1,0,3:T(8,128)} async-done(((f32[2,2,16,128,512]{4,2,1,0,3:T(8,128)}), f32[2,2,16,128,512]{4,2,1,0,3:T(8,128)}, u32[]{:S(2)}, u32[]{:S(2)}) %all-to-all-start.5) | async-done | bytes 16777248 | tf_op jit(solution)/shard_map/all_to_all | solution.py:159
  1334.5 323.9 %all-to-all-done.2 = f32[2,2,16,128,512]{4,2,1,0,3:T(8,128)} async-done(((f32[2,2,16,128,512]{4,2,1,0,3:T(8,128)}), f32[2,2,16,128,512]{4,2,1,0,3:T(8,128)}, u32[]{:S(2)}, u32[]{:S(2)}) %all-to-all-start.2) | async-done | bytes 16777248 | tf_op jit(solution)/shard_map/all_to_all | solution.py:159
  1710.7 33.1 %fusion.22 = f32[2,2,16,16,64,128]{5,4,3,2,1,0:T(8,128)} fusion(f32[2,2,16,16,32,128]{5,4,3,2,1,0:T(8,128)} %get-tuple-element.47, f32[1,32,2,64]{3,1,0,2:T(8,128)S(1)} %get-tuple-element.49, f32[1,32,2,64]{3,1,0,2:T(8,128)S(1)} %get-tuple-element.48), kind=kOutput, calls=%fused_computation.33 | convolution fusion | flops 6442459136 | bytes 50364416 | tf_op jit(solution)/shard_map/pnyzab,pasc->snyzcb/dot_general | solution.py:111
  1743.9 31.5 %fusion.19 = f32[2,2,16,16,64,128]{5,4,3,2,1,0:T(8,128)} fusion(f32[2,2,16,16,32,128]{5,4,3,2,1,0:T(8,128)S(1)} %get-tuple-element.46, f32[1,32,2,64]{3,1,0,2:T(8,128)S(1)} %get-tuple-element.49, f32[1,32,2,64]{3,1,0,2:T(8,128)S(1)} %get-tuple-element.48), kind=kOutput, calls=%fused_computation.32 | convolution fusion | flops 6442459136 | bytes 50364416 | tf_op jit(solution)/shard_map/pnyzab,pasc->snyzcb/dot_general | solution.py:111
  1775.4 44.0 %multiply_subtract_fusion.1 = (f32[1,2,16,16,64,128]{5,4,3,2,1,0:T(8,128)}, f32[1,2,16,16,64,128]{5,4,3,2,1,0:T(8,128)}, f32[1,2,16,16,64,128]{5,4,3,2,1,0:T(8,128)}, f32[1,2,16,16,64,128]{5,4,3,2,1,0:T(8,128)}) fusion(f32[2,2,16,16,64,128]{5,4,3,2,1,0:T(8,128)} %fusion.19, f32[64,128]{1,0:T(8,128)S(1)} %copy-done.11, f32[64,128]{1,0:T(8,128)S(1)} %copy-done.13, ...), kind=kLoop, calls=%fused_computation.31 | loop fusion | flops 50331648 | bytes 134283264 | tf_op jit(solution)/shard_map/sub | solution.py:71
  1819.4 38.9 %fusion.2 = f32[2,16,16,64,128,1]{4,3,1,0,2,5:T(8,128)S(1)} fusion(f32[1,128,2,128]{1,3,0,2:T(8,128)S(1)} %copy-done.3, f32[1,128,2,128]{1,3,0,2:T(8,128)S(1)} %copy-done.5, f32[1,2,16,16,64,128]{5,4,3,2,1,0:T(8,128)} %get-tuple-element.6, f32[1,2,16,16,64,128]{5,4,3,2,1,0:T(8,128)} %get-tuple-element.5), kind=kOutput, calls=%fused_computation.4 | convolution fusion | flops 12893323264 | bytes 50593792 | tf_op jit(solution)/shard_map/pnyzcb,pbd->nyzcd/dot_general | solution.py:120
  1864.6 38.6 %fusion = f32[2,16,16,64,128,1]{4,3,1,0,2,5:T(8,128)S(1)} fusion(f32[1,128,2,128]{1,3,0,2:T(8,128)S(1)} %copy-done.3, f32[1,128,2,128]{1,3,0,2:T(8,128)S(1)} %copy-done.5, f32[1,2,16,16,64,128]{5,4,3,2,1,0:T(8,128)} %get-tuple-element.29, f32[1,2,16,16,64,128]{5,4,3,2,1,0:T(8,128)} %get-tuple-element.30), kind=kOutput, calls=%fused_computation.2 | convolution fusion | flops 12893323264 | bytes 50593792 | tf_op jit(solution)/shard_map/pnyzcb,pbd->nyzcd/dot_general | solution.py:120
  1909.6 22.9 fusion.35
  1951.6 28.8 %copy.257 = f32[2,1,16,16,32,128]{3,2,0,5,4,1:T(8,128)} copy(f32[2,1,16,16,32,128]{5,4,3,2,0,1:T(8,128)} %fusion.148) | data formatting | bytes 16777216 | tf_op jit(solution)/shard_map/reshape | solution.py:179
  1980.3 58.8 %reshape.1395 = f32[8,1,262144]{2,1,0:T(1,128)} reshape(f32[4096,1,2,16,16]{4,3,2,1,0:T(8,128)} %bitcast.242) | data formatting | bytes 16777216
  2039.2 187.5 %all_to_all.150 = f32[8,1,262144]{2,1,0:T(1,128)} all-to-all(f32[8,1,262144]{2,1,0:T(1,128)} %reshape.1395), channel_id=1, replica_groups=mesh['row'=4,'col'=8] {'col'}, dimensions={0} | all-to-all | bytes 16777216 | tf_op jit(solution)/shard_map/all_to_all | solution.py:180
  2227.2 26.6 reduce
  2253.7 51.0 %reshape.1396 = f32[4096,1,2,16,16]{4,3,2,1,0:T(8,128)} reshape(f32[8,262144]{1,0:T(8,128)} %reduce) | data formatting | bytes 16777216
  2304.8 32.3 %copy.258 = f32[2,1,16,16,8,512]{5,4,3,2,0,1:T(8,128)} copy(f32[2,1,16,16,8,512]{3,2,0,5,4,1:T(8,128)} %bitcast.99) | data formatting | bytes 16777216 | tf_op jit(solution)/shard_map/all_to_all | solution.py:180
  2368.0 92.5 %all-to-all-done.7 = f32[2,1,512,16,128]{4,3,0,1,2:T(8,128)} async-done(((f32[2,1,512,16,128]{4,3,0,1,2:T(8,128)}), f32[2,1,512,16,128]{4,3,0,1,2:T(8,128)}, u32[]{:S(2)}, u32[]{:S(2)}) %all-to-all-start.7) | async-done | bytes 8388640 | tf_op jit(solution)/shard_map/all_to_all | solution.py:80
  2516.2 23.1 fusion.103
  2539.4 69.9 %all-to-all-done.8 = f32[2,1,128,64,128]{4,2,0,1,3:T(8,128)} async-done(((f32[2,1,128,64,128]{4,2,0,1,3:T(8,128)}), f32[2,1,128,64,128]{4,2,0,1,3:T(8,128)}, u32[]{:S(2)}, u32[]{:S(2)}) %all-to-all-start.8) | async-done | bytes 8388640 | tf_op jit(solution)/shard_map/all_to_all | solution.py:76
  2637.3 25.8 fusion.32
  (141 shorter events, 547.0 us)
Async XLA Ops:
  0.0 8.9 copy-start.16
  0.0 8.9 copy-start.18
  0.0 8.9 copy-start.20
  0.1 8.9 copy-start.22
  44.9 190.9 %all-to-all-start.3 = ((f32[2,2,512,16,128]{4,3,1,0,2:T(8,128)}), f32[2,2,512,16,128]{4,3,1,0,2:T(8,128)}, u32[]{:S(2)}, u32[]{:S(2)}) async-start(f32[2,2,512,16,128]{4,3,1,0,2:T(8,128)} %copy.250), calls=%async_computation.3 | async-start | bytes 33554432 | tf_op jit(solution)/shard_map/all_to_all | solution.py:80
  235.8 190.5 %all-to-all-start = ((f32[2,2,512,16,128]{4,3,1,0,2:T(8,128)}), f32[2,2,512,16,128]{4,3,1,0,2:T(8,128)}, u32[]{:S(2)}, u32[]{:S(2)}) async-start(f32[2,2,512,16,128]{4,3,1,0,2:T(8,128)} %copy.241), calls=%async_computation | async-start | bytes 33554432 | tf_op jit(solution)/shard_map/all_to_all | solution.py:80
  243.7 239.4 %copy-start.10 = (f32[64,128]{1,0:T(8,128)}, f32[64,128]{1,0:T(8,128)S(1)}, u32[]{:S(2)}) copy-start(f32[64,128]{1,0:T(8,128)S(1)} %get-tuple-element.56) | copy-start | bytes 98308
  243.7 239.4 %copy-start.12 = (f32[64,128]{1,0:T(8,128)}, f32[64,128]{1,0:T(8,128)S(1)}, u32[]{:S(2)}) copy-start(f32[64,128]{1,0:T(8,128)S(1)} %get-tuple-element.57) | copy-start | bytes 98308
  244.3 311.1 %copy-start.2 = (f32[1,128,2,128]{1,3,0,2:T(8,128)}, f32[1,128,2,128]{1,3,0,2:T(8,128)S(1)}, u32[]{:S(2)}) copy-start(f32[1,128,2,128]{1,3,0,2:T(8,128)S(1)} %get-tuple-element.33) | copy-start | bytes 393220
  244.3 311.1 %copy-start.4 = (f32[1,128,2,128]{1,3,0,2:T(8,128)}, f32[1,128,2,128]{1,3,0,2:T(8,128)S(1)}, u32[]{:S(2)}) copy-start(f32[1,128,2,128]{1,3,0,2:T(8,128)S(1)} %get-tuple-element.34) | copy-start | bytes 393220
  540.9 190.5 %all-to-all-start.4 = ((f32[2,2,128,64,128]{2,4,1,0,3:T(8,128)}), f32[2,2,128,64,128]{2,4,1,0,3:T(8,128)}, u32[]{:S(2)}, u32[]{:S(2)}) async-start(f32[2,2,128,64,128]{2,4,1,0,3:T(8,128)} %copy.188), calls=%async_computation.4 | async-start | bytes 33554432 | tf_op jit(solution)/shard_map/all_to_all | solution.py:76
  731.5 190.2 %all-to-all-start.1 = ((f32[2,2,128,64,128]{2,4,1,0,3:T(8,128)}), f32[2,2,128,64,128]{2,4,1,0,3:T(8,128)}, u32[]{:S(2)}, u32[]{:S(2)}) async-start(f32[2,2,128,64,128]{2,4,1,0,3:T(8,128)} %copy.174), calls=%async_computation.1 | async-start | bytes 33554432 | tf_op jit(solution)/shard_map/all_to_all | solution.py:76
  921.7 369.3 %all-to-all-start.5 = ((f32[2,2,16,128,512]{4,2,1,0,3:T(8,128)}), f32[2,2,16,128,512]{4,2,1,0,3:T(8,128)}, u32[]{:S(2)}, u32[]{:S(2)}) async-start(f32[2,2,16,128,512]{4,2,1,0,3:T(8,128)} %copy.191), calls=%async_computation.5 | async-start | bytes 33554432 | tf_op jit(solution)/shard_map/all_to_all | solution.py:159
  1291.0 367.5 %all-to-all-start.2 = ((f32[2,2,16,128,512]{4,2,1,0,3:T(8,128)}), f32[2,2,16,128,512]{4,2,1,0,3:T(8,128)}, u32[]{:S(2)}, u32[]{:S(2)}) async-start(f32[2,2,16,128,512]{4,2,1,0,3:T(8,128)} %copy.177), calls=%async_computation.2 | async-start | bytes 33554432 | tf_op jit(solution)/shard_map/all_to_all | solution.py:159
  1743.9 31.5 %copy-start.11 = (f32[64,128]{1,0:T(8,128)S(1)}, f32[64,128]{1,0:T(8,128)}, u32[]{:S(2)}) copy-start(f32[64,128]{1,0:T(8,128)} %copy-done.10) | copy-start | bytes 98308
  1743.9 31.5 %copy-start.13 = (f32[64,128]{1,0:T(8,128)S(1)}, f32[64,128]{1,0:T(8,128)}, u32[]{:S(2)}) copy-start(f32[64,128]{1,0:T(8,128)} %copy-done.12) | copy-start | bytes 98308
  1775.4 44.0 %copy-start.3 = (f32[1,128,2,128]{1,3,0,2:T(8,128)S(1)}, f32[1,128,2,128]{1,3,0,2:T(8,128)}, u32[]{:S(2)}) copy-start(f32[1,128,2,128]{1,3,0,2:T(8,128)} %copy-done.2) | copy-start | bytes 393220
  1775.4 44.0 %copy-start.5 = (f32[1,128,2,128]{1,3,0,2:T(8,128)S(1)}, f32[1,128,2,128]{1,3,0,2:T(8,128)}, u32[]{:S(2)}) copy-start(f32[1,128,2,128]{1,3,0,2:T(8,128)} %copy-done.4) | copy-start | bytes 393220
  1909.5 22.9 copy-start.8
  1909.6 22.9 copy-start.9
  1932.4 7.2 copy-start.14
  1932.4 7.2 copy-start.15
  2361.6 99.0 %all-to-all-start.7 = ((f32[2,1,512,16,128]{4,3,0,1,2:T(8,128)}), f32[2,1,512,16,128]{4,3,0,1,2:T(8,128)}, u32[]{:S(2)}, u32[]{:S(2)}) async-start(f32[2,1,512,16,128]{4,3,0,1,2:T(8,128)} %copy.202), calls=%async_computation.7 | async-start | bytes 16777216 | tf_op jit(solution)/shard_map/all_to_all | solution.py:80
  2510.1 99.2 %all-to-all-start.8 = ((f32[2,1,128,64,128]{4,2,0,1,3:T(8,128)}), f32[2,1,128,64,128]{4,2,0,1,3:T(8,128)}, u32[]{:S(2)}, u32[]{:S(2)}) async-start(f32[2,1,128,64,128]{4,2,0,1,3:T(8,128)} %copy.208), calls=%async_computation.8 | async-start | bytes 16777216 | tf_op jit(solution)/shard_map/all_to_all | solution.py:76
  (10 other events, 48.1 us)
where the time goes:
time: 2680 us; the launch traced here: 2660 us
  waiting for transfers between devices  1420 us (53%)
  local copies, waits for them, and re-layouts  460 us (17%)
  matrix products  289 us (11%)
  other arithmetic  248 us (9%)
  blocking collectives  187 us (7%)
  starting transfers between devices  53.6 us (2%)
    all_to_all x2, waiting for transfers between devices, to_grid(): lax.all_to_all(turned, 'col', split_axis=3, concat_axis=4, tiled=True)  646 us
    all_to_all x3, waiting for transfers between devices, row_pass(): lax.all_to_all(batched, 'row', split_axis=2, concat_axis=3, tiled=True)  420 us
    all_to_all x3, waiting for transfers between devices, back_rows(): lax.all_to_all(values, 'row', split_axis=3, concat_axis=2, tiled=True)  359 us
    all_to_all x1, blocking collectives, to_spectrum(): lax.all_to_all(flattened, 'col', split_axis=4, concat_axis=3, tiled=True)  187 us
    unnamed x58, local copies, waits for them, and re-layouts  126 us
    dot_general x2, matrix products, cols_inverse(): jnp.einsum('pnyzcb,pbd->nyzcd', section_one, real_table, precision=lax.Pr...  77.6 us
    sub x4, other arithmetic, rotate(): values[0] * cosine - values[1] * sine_part  76.8 us
    all_to_all x4, local copies, waits for them, and re-layouts, to_grid(): lax.all_to_all(turned, 'col', split_axis=3, concat_axis=4, tiled=True)  70.2 us
  transfers between devices with their start and end apart: 8, of which 8 were waited for; matrix products, arithmetic and copies ran while one was open for 8% of the time, Pallas kernels for 0%

commit v1 on v0

v1 whole, which is shorter than its diff:
```python
import math

import jax
import jax.numpy as jnp
from jax import lax
from jax.sharding import PartitionSpec as P

RADIX = 128


viscous_rate = 1.5
wave_scale = 3.0
series_terms = 12


def section_weights(wave_x, wave_y, length):
    square = wave_x * wave_x + wave_y * wave_y
    kappa_x = wave_scale * wave_x.astype(jnp.float32) / length
    kappa_y = wave_scale * wave_y.astype(jnp.float32) / length
    kappa_sq = kappa_x * kappa_x + kappa_y * kappa_y
    zvalue = -viscous_rate * kappa_sq
    damping = jnp.exp(zvalue)
    near_zero = 27 * square < 2 * length * length

    def series(degree):
        running = jnp.full_like(zvalue, 1.0 / math.factorial(series_terms - 1 + degree))
        for term_index in range(series_terms - 2, -1, -1):
            running = running * zvalue + 1.0 / math.factorial(term_index + degree)
        return running

    clamped = jnp.where(near_zero, -1.0, zvalue)
    exp_clamped = jnp.exp(clamped)
    closed_one = (exp_clamped - 1.0) / clamped
    closed_two = (exp_clamped - 1.0 - clamped) / (clamped * clamped)
    closed_three = (exp_clamped - 1.0 - clamped - 0.5 * clamped * clamped) / (
        clamped * clamped * clamped
    )
    phi_one = jnp.where(near_zero, series(1), closed_one)
    phi_two = jnp.where(near_zero, series(2), closed_two)
    phi_three = jnp.where(near_zero, series(3), closed_three)
    weight_a = phi_one - 3.0 * phi_two + 4.0 * phi_three
    weight_b = phi_two - 2.0 * phi_three
    weight_c = 4.0 * phi_three - phi_two
    keep_mask = ((3 * jnp.abs(wave_x) < length) & (3 * jnp.abs(wave_y) < length)).astype(
        jnp.float32
    )
    inverse_sq = length * length / (9.0 * jnp.maximum(square, 1).astype(jnp.float32))
    return (damping, weight_a, weight_b, weight_c, kappa_x, kappa_y, keep_mask, inverse_sq)


def section_table(count_in, count_out, period, direction):
    row_ids = lax.broadcasted_iota(jnp.int32, (count_in, count_out), 0)
    col_ids = lax.broadcasted_iota(jnp.int32, (count_in, count_out), 1)
    angles = direction * 2.0 * math.pi / period * (row_ids * col_ids % period).astype(jnp.float32)
    cosine = jnp.cos(angles)
    sine_part = jnp.sin(angles)
    return jnp.stack(
        [jnp.stack([cosine, sine_part], axis=1), jnp.stack([-sine_part, cosine], axis=1)], axis=0
    )


def twiddle(count_c, count_b, period, direction):
    row_ids = lax.broadcasted_iota(jnp.int32, (count_c, count_b), 0)
    col_ids = lax.broadcasted_iota(jnp.int32, (count_c, count_b), 1)
    angles = direction * 2.0 * math.pi / period * (row_ids * col_ids % period).astype(jnp.float32)
    return (jnp.cos(angles), jnp.sin(angles))


def rotate(values, cosine, sine_part):
    return jnp.stack(
        [values[0] * cosine - values[1] * sine_part, values[0] * sine_part + values[1] * cosine]
    )


def product(equation, left, right):
    return jnp.einsum(equation, left, right, precision=lax.Precision.HIGH)


def lines_inverse(pieces):
    parts, count_k, length = pieces.shape
    count_b = RADIX
    count_a = length // count_b
    shaped = pieces.reshape((parts, count_k, count_a, count_b))
    first = product("pkab,pasc->skcb", shaped, section_table(count_a, count_a, count_a, 1.0))
    first = rotate(first, *twiddle(count_a, count_b, length, 1.0))
    second = product("pkcb,pbsd->skcd", first, section_table(count_b, count_b, count_b, 1.0))
    return second.reshape((parts, count_k, length))


def lines_forward(pieces):
    parts, count_k, length = pieces.shape
    count_d = RADIX
    count_c = length // count_d
    shaped = pieces.reshape((parts, count_k, count_c, count_d))
    first = product("pkcd,pdsf->skcf", shaped, section_table(count_d, count_d, count_d, -1.0))
    first = rotate(first, *twiddle(count_c, count_d, length, -1.0))
    second = product("pkcf,pcse->skef", first, section_table(count_c, count_c, count_c, -1.0))
    return second.reshape((parts, count_k, length))


def turned_table(count_c, count_b, period, direction):
    c_ids = lax.broadcasted_iota(jnp.int32, (count_c, count_b, count_b), 0)
    b_ids = lax.broadcasted_iota(jnp.int32, (count_c, count_b, count_b), 1)
    d_ids = lax.broadcasted_iota(jnp.int32, (count_c, count_b, count_b), 2)
    steps = b_ids * (c_ids + count_c * d_ids) % period
    angles = direction * 2.0 * math.pi / period * steps.astype(jnp.float32)
    return jnp.cos(angles), jnp.sin(angles)


def columns_inverse(pieces, table):
    parts, half_count, count_y = pieces.shape
    count_a = half_count // RADIX
    count_c = 2 * count_a
    shaped = pieces.reshape((parts, count_a, RADIX, count_y))
    first = product("paby,pasc->csby", shaped, section_table(count_a, count_c, count_c, 1.0))
    return product("csby,csbd->cdy", first, table)


def columns_forward(grid, table):
    count_c, count_d, count_y = grid.shape
    half_count = count_c // 2
    first = product("cdy,cpfd->cpfy", grid, table)
    second = product(
        "cpfy,pcse->sefy", first, section_table(count_c, half_count, count_c, -1.0)
    )
    return second.reshape((2, half_count * count_d, count_y))


def to_columns(lines):
    return lax.all_to_all(lines, ("col", "row"), split_axis=2, concat_axis=1, tiled=True)


def to_lines(columns):
    return lax.all_to_all(columns, ("col", "row"), split_axis=1, concat_axis=2, tiled=True)


def positions(shape, start_x, start_y, length):
    wave_x = start_x + lax.broadcasted_iota(jnp.int32, shape, 0)
    index_y = start_y + lax.broadcasted_iota(jnp.int32, shape, 1)
    wave_y = jnp.where(index_y < length // 2, index_y, index_y - length)
    return wave_x, wave_y


def nonlinear(section_field, length):
    block_x = section_field.shape[1]
    lines = lax.all_to_all(section_field, "row", split_axis=1, concat_axis=2, tiled=True)
    count_k = lines.shape[1]
    start_x = lax.axis_index("col") * block_x + lax.axis_index("row") * count_k
    wave_x, wave_y = positions((count_k, length), start_x, 0, length)
    square = wave_x * wave_x + wave_y * wave_y
    kappa_x = wave_scale * wave_x.astype(jnp.float32) / length
    kappa_y = wave_scale * wave_y.astype(jnp.float32) / length
    keep = (3 * jnp.abs(wave_x) < length) & (3 * jnp.abs(wave_y) < length)
    doubled = jnp.where(wave_x == 0, 1.0, 2.0) * (1.0 / length)
    inverse_sq = length * length / (9.0 * jnp.maximum(square, 1).astype(jnp.float32))
    factor = jnp.where(keep, inverse_sq * doubled, 0.0)
    scale_u = kappa_y * factor
    scale_v = kappa_x * factor
    spec_u = jnp.stack([-scale_u * lines[1], scale_u * lines[0]])
    spec_v = jnp.stack([scale_v * lines[1], -scale_v * lines[0]])
    count_c = length // RADIX
    cosine, sine_part = turned_table(count_c, RADIX, length, 1.0)
    table = jnp.stack([cosine, -sine_part], axis=1)
    vel_u = columns_inverse(to_columns(lines_inverse(spec_u)), table)
    vel_v = columns_inverse(to_columns(lines_inverse(spec_v)), table)
    cross = lines_forward(to_lines(columns_forward(vel_u * vel_v, table)))
    square_gap = lines_forward(
        to_lines(columns_forward((vel_v - vel_u) * (vel_v + vel_u), table))
    )
    scale = jnp.where(keep, 1.0 / length, 0.0)
    weight_cross = (kappa_x * kappa_x - kappa_y * kappa_y) * scale
    weight_gap = kappa_x * kappa_y * scale
    term = weight_cross * cross + weight_gap * square_gap
    return lax.all_to_all(term, "row", split_axis=2, concat_axis=1, tiled=True)


def per_device(start_field, section_field, start_term, first_term, second_term):
    members = start_field.shape[0]
    block_x = start_field.shape[2]
    block_y = start_field.shape[3]
    length = block_y * lax.axis_size("row")
    wave_x, wave_y = positions(
        (block_x, block_y),
        lax.axis_index("col") * block_x,
        lax.axis_index("row") * block_y,
        length,
    )
    damping, weight_a, weight_b, weight_c = section_weights(wave_x, wave_y, length)[:4]
    linear = (
        damping * start_field
        + weight_a * start_term
        + 2.0 * weight_b * (first_term + second_term)
    )
    linear, weight_c = lax.optimization_barrier((linear, weight_c))
    section_term = jnp.stack([nonlinear(section_field[m], length) for m in range(members)])
    return linear + weight_c * section_term


def solution(mesh):
    return jax.shard_map(
        per_device,
        mesh=mesh,
        in_specs=(
            P(None, None, "col", "row"),
            P(None, None, "col", "row"),
            P(None, None, "col", "row"),
            P(None, None, "col", "row"),
            P(None, None, "col", "row"),
        ),
        out_specs=P(None, None, "col", "row"),
        check_vma=False,
    )
```

time: 2680 us -> 1410 us (0.53)
  waiting for transfers between devices: 1420 us -> 720 us
  blocking collectives: 187 us -> 0 us
  local copies, waits for them, and re-layouts: 460 us -> 285 us
  other arithmetic: 248 us -> 137 us
  matrix products: 289 us -> 211 us
    all_to_all x8 -> x6, waiting for transfers between devices: 1420 us -> 720 us  [the longest x2 296 us: to_columns(): lax.all_to_all(lines, ('col', 'row'), split_axis=2, concat_axis=1, tiled=...]
    all_to_all x1 -> x0, blocking collectives: 187 us -> none  [to_spectrum(): lax.all_to_all(flattened, 'col', split_axis=4, concat_axis=3, tiled=True)]
    unnamed x58 -> x13, local copies, waits for them, and re-layouts: 126 us -> 15.4 us
    all_to_all x13 -> x8, local copies, waits for them, and re-layouts: 188 us -> 78.8 us  [the longest x4 32.6 us: to_lines(): lax.all_to_all(columns, ('col', 'row'), split_axis=1, concat_axis=2, tile...]
    reshape x1 -> x6, local copies, waits for them, and re-layouts: 28.8 us -> 129 us  [the longest x2 63 us: lines_inverse(): return second.reshape((parts, count_k, length))]
    dot_general x12 -> x16, matrix products: 289 us -> 211 us  [product(): return jnp.einsum(equation, left, right, precision=lax.Precision.HIGH)]
    transpose x6 -> x0, local copies, waits for them, and re-layouts: 71.6 us -> none  [the longest x2 40.5 us: to_grid(): turned = jnp.transpose(columns, (0, 1, 3, 4, 2))]
    sub x4 -> x2, other arithmetic: 76.8 us -> 11.4 us  [rotate(): values[0] * cosine - values[1] * sine_part]
  transfers between devices with their start and end apart: 8 -> 6, of which waited for: 8 -> 6; matrix products, arithmetic and copies ran while one was open for 8% -> 15% of each run, Pallas kernels for 0% -> 0%
where the time goes in v1:
time: 1410 us; the launch traced here: 1390 us
  waiting for transfers between devices  720 us (51%)
  local copies, waits for them, and re-layouts  285 us (20%)
  matrix products  211 us (15%)
  other arithmetic  137 us (10%)
  starting transfers between devices  40.8 us (3%)
    all_to_all x2, waiting for transfers between devices, to_columns(): lax.all_to_all(lines, ('col', 'row'), split_axis=2, concat_axis=1, tiled=...  296 us
    all_to_all x2, waiting for transfers between devices, to_lines(): lax.all_to_all(columns, ('col', 'row'), split_axis=1, concat_axis=2, tile...  284 us
    dot_general x16, matrix products, product(): return jnp.einsum(equation, left, right, precision=lax.Precision.HIGH)  211 us
    all_to_all x1, waiting for transfers between devices, nonlinear(): lax.all_to_all(section_field, 'row', split_axis=1, concat_axis=2, tiled=T...  91.7 us
    reshape x2, local copies, waits for them, and re-layouts, lines_inverse(): return second.reshape((parts, count_k, length))  63 us
    all_to_all x1, waiting for transfers between devices, nonlinear(): return lax.all_to_all(term, 'row', split_axis=2, concat_axis=1, tiled=True)  48.2 us
    reshape x2, local copies, waits for them, and re-layouts, columns_forward(): return second.reshape((2, half_count * count_d, count_y))  46.9 us
    all_to_all x4, local copies, waits for them, and re-layouts, to_lines(): lax.all_to_all(columns, ('col', 'row'), split_axis=1, concat_axis=2, tile...  32.6 us
  transfers between devices with their start and end apart: 6, of which 6 were waited for; matrix products, arithmetic and copies ran while one was open for 15% of the time, Pallas kernels for 0%

profile of v1, /device:TPU:0, one launch (start us, length us, event | category | flops | bytes accessed | tf_op | source)
XLA Modules:
  0.0 1394.6 jit_solution(14746386528013879035)
XLA Ops:
  0.0 15.4 %copy.229 = f32[1,2,512,2048]{3,1,2,0:T(2,128)} copy(f32[1,2,512,2048]{3,2,1,0:T(8,128)} %param.6) | data formatting | bytes 16777216 | tf_op args[1]
  23.2 91.7 %all-to-all-done = f32[2,512,2048]{2,0,1:T(2,128)} async-done(((f32[2,512,2048]{2,0,1:T(2,128)}), f32[2,512,2048]{2,0,1:T(2,128)}, u32[]{:S(2)}, u32[]{:S(2)}) %all-to-all-start) | async-done | bytes 8388640 | tf_op jit(solution)/shard_map/all_to_all | solution.py:146
  183.1 31.3 %copy.115 = f32[2,128,8192]{1,0,2:T(2,128)} copy(f32[2,128,8192]{1,2,0:T(8,128)S(1)} %bitcast.248) | data formatting | bytes 16777216 | tf_op jit(solution)/shard_map/reshape | solution.py:87
  232.9 31.7 %copy.119 = f32[2,128,8192]{1,0,2:T(2,128)} copy(f32[2,128,8192]{1,2,0:T(8,128)S(1)} %bitcast.247) | data formatting | bytes 16777216 | tf_op jit(solution)/shard_map/reshape | solution.py:87
  264.6 140.9 %all-to-all-done.1 = f32[2,128,8192]{1,0,2:T(2,128)} async-done(((f32[2,128,8192]{1,0,2:T(2,128)}), f32[2,128,8192]{1,0,2:T(2,128)}, u32[]{:S(2)}, u32[]{:S(2)}) %all-to-all-start.1) | async-done | bytes 8388640 | tf_op jit(solution)/shard_map/all_to_all | solution.py:130
  413.6 19.0 %fusion.171 = (f32[64,1,128,128]{2,3,1,0:T(8,128)}, f32[64,1,128,128]{2,3,1,0:T(8,128)}) fusion(s32[128]{0:T(128)S(1)} %iota_multiply_fusion), kind=kLoop, calls=%fused_computation.198 | loop fusion | flops 16777216 | bytes 8389120 | tf_op jit(solution)/shard_map/cos | solution.py:107
  443.1 155.3 %all-to-all-done.2 = f32[2,128,8192]{1,0,2:T(2,128)} async-done(((f32[2,128,8192]{1,0,2:T(2,128)}), f32[2,128,8192]{1,0,2:T(2,128)}, u32[]{:S(2)}, u32[]{:S(2)}) %all-to-all-start.2) | async-done | bytes 8388640 | tf_op jit(solution)/shard_map/all_to_all | solution.py:130
  608.8 14.3 %fusion.42 = f32[64,2,128,256]{3,0,2,1:T(8,128)} fusion(f32[2,128,32,256]{3,2,0,1:T(8,128)} %copy.176, f32[1,32,2,64]{3,1,0,2:T(8,128)S(1)} %get-tuple-element.46, f32[1,32,2,64]{3,1,0,2:T(8,128)S(1)} %get-tuple-element.45), kind=kOutput, calls=%fused_computation.59 | convolution fusion | flops 1610620928 | bytes 25198592 | tf_op jit(solution)/shard_map/paby,pasc->csby/dot_general | solution.py:76
  633.0 27.8 %fusion.8 = f32[64,128,256,1]{2,1,3,0:T(8,128)} fusion(f32[64,2,128,256]{3,0,2,1:T(8,128)} %fusion.42, f32[64,1,128,128]{2,3,1,0:T(8,128)} %get-tuple-element.48, f32[64,1,128,128]{2,3,1,0:T(8,128)} %get-tuple-element.47), kind=kOutput, calls=%fused_computation.8 | convolution fusion | flops 3223322624 | bytes 33554432 | tf_op jit(solution)/shard_map/csby,csbd->cdy/dot_general | solution.py:76
  660.7 27.7 %fusion.6 = f32[64,128,256,1]{2,1,3,0:T(8,128)} fusion(f32[64,2,128,256]{3,0,2,1:T(8,128)} %fusion.45, f32[64,1,128,128]{2,3,1,0:T(8,128)} %get-tuple-element.48, f32[64,1,128,128]{2,3,1,0:T(8,128)} %get-tuple-element.47), kind=kOutput, calls=%fused_computation.6 | convolution fusion | flops 3223322624 | bytes 33554432 | tf_op jit(solution)/shard_map/csby,csbd->cdy/dot_general | solution.py:76
  688.5 15.4 %fusion.16 = f32[64,2,128,256]{3,2,1,0:T(8,128)} fusion(f32[64,128,256,1]{2,1,3,0:T(8,128)} %fusion.6, f32[64,128,256,1]{2,1,3,0:T(8,128)} %fusion.8, f32[64,1,128,128]{2,3,1,0:T(8,128)} %get-tuple-element.48, f32[64,1,128,128]{2,3,1,0:T(8,128)} %get-tuple-element.47), kind=kOutput, calls=%fused_computation.23 | convolution fusion | flops 3229614080 | bytes 41943040 | tf_op jit(solution)/shard_map/cdy,cpfd->cpfy/dot_general | solution.py:76
  703.9 20.8 %fusion.168 = f32[2,32,128,256]{3,1,2,0:T(8,128)S(1)} fusion(f32[64,2,128,256]{3,2,1,0:T(8,128)} %fusion.16, f32[1,64,2,32]{1,3,0,2:T(8,128)S(1)} %get-tuple-element.44, f32[1,64,2,32]{1,3,0,2:T(8,128)S(1)} %get-tuple-element.43), kind=kOutput, calls=%fused_computation.197 | convolution fusion | flops 1610620928 | bytes 25198592 | tf_op jit(solution)/shard_map/cpfy,pcse->sefy/dot_general | solution.py:76
  729.6 23.5 %copy.135 = f32[2,4096,256]{2,0,1:T(2,128)} copy(f32[2,4096,256]{2,1,0:T(8,128)S(1)} %bitcast.252) | data formatting | bytes 16777216 | tf_op jit(solution)/shard_map/reshape | solution.py:126
  760.8 15.1 %fusion.18 = f32[64,2,128,256]{3,2,1,0:T(8,128)} fusion(f32[64,128,256,1]{2,1,3,0:T(8,128)} %fusion.6, f32[64,128,256,1]{2,1,3,0:T(8,128)} %fusion.8, f32[64,1,128,128]{2,3,1,0:T(8,128)} %get-tuple-element.48, f32[64,1,128,128]{2,3,1,0:T(8,128)} %get-tuple-element.47), kind=kOutput, calls=%fused_computation.25 | convolution fusion | flops 3225419776 | bytes 41943040 | tf_op jit(solution)/shard_map/cdy,cpfd->cpfy/dot_general | solution.py:76
  775.9 21.2 %fusion.165 = f32[2,32,128,256]{3,1,2,0:T(8,128)S(1)} fusion(f32[64,2,128,256]{3,2,1,0:T(8,128)} %fusion.18, f32[1,64,2,32]{1,3,0,2:T(8,128)S(1)} %get-tuple-element.44, f32[1,64,2,32]{1,3,0,2:T(8,128)S(1)} %get-tuple-element.43), kind=kOutput, calls=%fused_computation.196 | convolution fusion | flops 1610620928 | bytes 25198592 | tf_op jit(solution)/shard_map/cpfy,pcse->sefy/dot_general | solution.py:76
  801.9 23.4 %copy.125 = f32[2,4096,256]{2,0,1:T(2,128)} copy(f32[2,4096,256]{2,1,0:T(8,128)S(1)} %bitcast.253) | data formatting | bytes 16777216 | tf_op jit(solution)/shard_map/reshape | solution.py:126
  825.4 120.6 %all-to-all-done.4 = f32[2,4096,256]{2,0,1:T(2,128)} async-done(((f32[2,4096,256]{2,0,1:T(2,128)}), f32[2,4096,256]{2,0,1:T(2,128)}, u32[]{:S(2)}, u32[]{:S(2)}) %all-to-all-start.4) | async-done | bytes 8388640 | tf_op jit(solution)/shard_map/all_to_all | solution.py:134
  975.8 163.2 %all-to-all-done.3 = f32[2,4096,256]{2,0,1:T(2,128)} async-done(((f32[2,4096,256]{2,0,1:T(2,128)}), f32[2,4096,256]{2,0,1:T(2,128)}, u32[]{:S(2)}, u32[]{:S(2)}) %all-to-all-start.3) | async-done | bytes 8388640 | tf_op jit(solution)/shard_map/all_to_all | solution.py:134
  1255.1 13.1 copy.142
  1274.2 23.9 %multiply_subtract_fusion.4 = (f32[512,2048]{1,0:T(8,128)}, f32[512,2048]{1,0:T(8,128)}, f32[512,2048]{1,0:T(8,128)}, f32[512,2048]{1,0:T(8,128)}) fusion(f32[512]{0:T(512)S(1)} %multiply_multiply_fusion.3, s32[2048]{0:T(1024)S(1)} %get-tuple-element.50, s32[2048]{0:T(1024)S(1)} %get-tuple-element.49, pred[2048]{0:T(1024)(128)(4,1)S(1)} %fusion.214, ...), kind=kLoop, calls=%fused_computation.188 | loop fusion | flops 102760448 | bytes 16799744 | tf_op jit(solution)/shard_map/sub | solution.py:43
  1298.1 21.0 %multiply_add_fusion.2 = f32[1,2,512,2048]{3,2,1,0:T(8,128)} fusion(f32[1,2,512,2048]{3,2,1,0:T(8,128)} %param.8, f32[1,2,512,2048]{3,2,1,0:T(8,128)} %param.9, f32[1,2,512,2048]{3,2,1,0:T(8,128)} %param.7, f32[1,2,512,2048]{3,2,1,0:T(8,128)} %param.5, f32[512,2048]{1,0:T(8,128)} %get-tuple-element.40, f32[512,2048]{1,0:T(8,128)} %get-tuple-element.41, ...), kind=kLoop, calls=%fused_computation.55 | loop fusion | flops 12582912 | bytes 54525952 | tf_op jit(solution)/shard_map/add | solution.py:190
  1319.1 48.2 %all-to-all-done.5 = f32[2,128,8192]{1,0,2:T(2,128)} async-done(((f32[2,128,8192]{1,0,2:T(2,128)}), f32[2,128,8192]{1,0,2:T(2,128)}, u32[]{:S(2)}, u32[]{:S(2)}) %all-to-all-start.5) | async-done | bytes 8388640 | tf_op jit(solution)/shard_map/all_to_all | solution.py:174
  1367.3 13.2 copy.143
  1380.4 13.7 multiply_add_fusion
  (85 shorter events, 302.5 us)
Async XLA Ops:
  15.4 99.6 %all-to-all-start = ((f32[2,512,2048]{2,0,1:T(2,128)}), f32[2,512,2048]{2,0,1:T(2,128)}, u32[]{:S(2)}, u32[]{:S(2)}) async-start(f32[2,512,2048]{2,0,1:T(2,128)} %bitcast.250), calls=%async_computation | async-start | bytes 16777216 | tf_op jit(solution)/shard_map/all_to_all | solution.py:146
  21.1 128.1 %copy-start.2 = (pred[128]{0:T(512)(128)(4,1)}, pred[128]{0:T(512)(128)(4,1)S(1)}, u32[]{:S(2)}) copy-start(pred[128]{0:T(512)(128)(4,1)S(1)} %multiply_compare_fusion.1) | copy-start | bytes 388
  214.4 191.1 %all-to-all-start.1 = ((f32[2,128,8192]{1,0,2:T(2,128)}), f32[2,128,8192]{1,0,2:T(2,128)}, u32[]{:S(2)}, u32[]{:S(2)}) async-start(f32[2,128,8192]{1,0,2:T(2,128)} %copy.115), calls=%async_computation.1 | async-start | bytes 16777216 | tf_op jit(solution)/shard_map/all_to_all | solution.py:130
  405.5 192.9 %all-to-all-start.2 = ((f32[2,128,8192]{1,0,2:T(2,128)}), f32[2,128,8192]{1,0,2:T(2,128)}, u32[]{:S(2)}, u32[]{:S(2)}) async-start(f32[2,128,8192]{1,0,2:T(2,128)} %copy.119), calls=%async_computation.2 | async-start | bytes 16777216 | tf_op jit(solution)/shard_map/all_to_all | solution.py:130
  608.7 14.3 %copy-start.1 = (f32[2,128,32,256]{3,2,0,1:T(8,128)S(1)}, f32[2,128,32,256]{3,2,0,1:T(8,128)}, u32[]{:S(2)}) copy-start(f32[2,128,32,256]{3,2,0,1:T(8,128)} %copy.177) | copy-start | bytes 25165828
  753.1 192.9 %all-to-all-start.4 = ((f32[2,4096,256]{2,0,1:T(2,128)}), f32[2,4096,256]{2,0,1:T(2,128)}, u32[]{:S(2)}, u32[]{:S(2)}) async-start(f32[2,4096,256]{2,0,1:T(2,128)} %copy.135), calls=%async_computation.4 | async-start | bytes 16777216 | tf_op jit(solution)/shard_map/all_to_all | solution.py:134
  825.4 129.5 %copy-start.3 = (pred[128]{0:T(512)(128)(4,1)S(1)}, pred[128]{0:T(512)(128)(4,1)}, u32[]{:S(2)}) copy-start(pred[128]{0:T(512)(128)(4,1)} %copy-done.2) | copy-start | bytes 388
  825.4 129.5 %copy-start.4 = (f32[128]{0:T(128)S(1)}, f32[128]{0:T(128)}, u32[]{:S(2)}) copy-start(f32[128]{0:T(128)} %get-tuple-element.52) | copy-start | bytes 1540
  825.4 129.5 %copy-start.5 = (f32[128]{0:T(128)S(1)}, f32[128]{0:T(128)}, u32[]{:S(2)}) copy-start(f32[128]{0:T(128)} %get-tuple-element.54) | copy-start | bytes 1540
  946.0 193.0 %all-to-all-start.3 = ((f32[2,4096,256]{2,0,1:T(2,128)}), f32[2,4096,256]{2,0,1:T(2,128)}, u32[]{:S(2)}, u32[]{:S(2)}) async-start(f32[2,4096,256]{2,0,1:T(2,128)} %copy.125), calls=%async_computation.3 | async-start | bytes 16777216 | tf_op jit(solution)/shard_map/all_to_all | solution.py:134
  1155.4 6.8 copy-start
  1268.2 99.1 %all-to-all-start.5 = ((f32[2,128,8192]{1,0,2:T(2,128)}), f32[2,128,8192]{1,0,2:T(2,128)}, u32[]{:S(2)}, u32[]{:S(2)}) async-start(f32[2,128,8192]{1,0,2:T(2,128)} %copy.142), calls=%async_computation.5 | async-start | bytes 16777216 | tf_op jit(solution)/shard_map/all_to_all | solution.py:174
